TPU v7x, 256 devices: a whole 4x4x8 slice. The times are simulated.
256 devices in a mesh: gx: 8 (over y, core), gy: 32 (over z, x).
Axes of the slice: x: 4, y: 4, z: 8, core: 2. Of those that a mesh axis runs over, the one named last changes fastest.
Arguments:
- pressure: float32 [512, 512, 512], P('gx', 'gy'), may hold values from -6 to 6
- divergence: float32 [512, 512, 512], P('gx', 'gy'), may hold values from -6 to 6
- diagonal: float32 [512, 512, 512], P('gx', 'gy'), may hold values from 0.05 to 0.5
- normals: float32 [3, 262144], P(None, ('gx', 'gy')), may hold values from -6 to 6
- traction: float32 [3, 262144], P(None, ('gx', 'gy')), may hold values from -3 to 3
- slot_of: int32 [8, 32768], P('gx'), may hold values from 0 to 98303, as said below
- counts: int32 [256], P(('gx', 'gy')), may hold values from 0 to 3072, as said below
- previous: float32 [3, 786432], P(None, ('gx', 'gy')), may hold values from -6 to 6
- secant_v: float32 [32, 3, 786432], P(None, None, ('gx', 'gy')), may hold values from -6 to 6
- secant_w: float32 [32, 3, 786432], P(None, None, ('gx', 'gy')), may hold values from -940.60406 to 940.60406
Outputs:
- pressure_new: float32 [512, 512, 512], P('gx', 'gy')
- coupled: float32 [3, 786432], P(None, ('gx', 'gy'))
Inputs may be any that keep to these rules, and one draw needn't show every extreme that they name: Within each group (row of slot_of) the places are distinct; place o * 3072 + s has s < counts[a * 32 + o]; every such place is used; the rows of one device (aligned blocks of 1024 entries) send at most 96 rows to one owner, and exactly 96 to some owner. The counts of one group sum to 32768; some owner of every group holds exactly 3072.
All inputs are finite; a program needn't handle non-finite values.
Results may differ from a plain program's by a relative error of at most 0.00019.
Values sent between devices are 32-bit elements; how exact they have to be, the bound alone decides.
A program may use at most 128 MiB of HBM per device.

v0:
```python
import jax
import jax.numpy as jnp
from jax import lax
from jax.sharding import PartitionSpec as P

SWEEPS = 2


def extended(cells, sides, width):
    for axis, dim in sides:
        count = lax.axis_size(axis)
        ends = count - 1
        head = lax.slice_in_dim(cells, 0, width, axis=dim)
        tail = lax.slice_in_dim(cells, cells.shape[dim] - width, cells.shape[dim], axis=dim)
        cells = jnp.concatenate(
            [
                lax.ppermute(tail, axis, [(i, (i + 1) % count) for i in range(ends)]),
                cells,
                lax.ppermute(head, axis, [((i + 1) % count, i) for i in range(ends)]),
            ],
            axis=dim,
        )
    return cells


def stencil_sum(padded):
    padded = jnp.pad(padded, ((0, 0), (0, 0), (1, 1)))
    total = padded[2:, 1:-1, 1:-1] + padded[:-2, 1:-1, 1:-1]
    total = total + padded[1:-1, 2:, 1:-1] + padded[1:-1, :-2, 1:-1]
    total = total + padded[1:-1, 1:-1, 2:] + padded[1:-1, 1:-1, :-2]
    return total


def sweep_once(field, divergence, diagonal):
    padded = extended(field, (("gx", 0), ("gy", 1)), 1)
    return (divergence + stencil_sum(padded)) / (6.0 + diagonal)


def shards(
    pressure, divergence, diagonal, normals, traction, slot_of, counts, previous, secant_v, secant_w
):
    columns = secant_v.shape[0]
    capacity = previous.shape[1]
    slot_index = jnp.arange(capacity, dtype=jnp.int32)
    occupied = (slot_index < counts[0]).astype(jnp.float32)
    masked_v = (secant_v * occupied[None, None, :]).reshape(columns, 3 * capacity)
    gram_local = jnp.dot(masked_v, masked_v.T, precision=lax.Precision.HIGHEST)
    field = pressure
    for sweep_index in range(SWEEPS):
        field = sweep_once(field, divergence, diagonal)
    surface = field[:, :, -1].reshape(-1)
    forces = normals * surface[None, :] + traction
    own_index = lax.axis_index("gy")
    all_slots = slot_of[0]
    gathered = lax.all_gather(forces, "gy", axis=1, tiled=True)
    placed = jnp.where(all_slots // capacity == own_index, all_slots % capacity, capacity)
    owned = jnp.zeros((3, capacity), jnp.float32).at[:, placed].set(gathered, mode="drop")
    residual = occupied[None, :] * (owned - previous)
    projection_local = jnp.dot(
        masked_v, residual.reshape(3 * capacity), precision=lax.Precision.HIGHEST
    )
    gram, projection = lax.psum((gram_local, projection_local), ("gx", "gy"))
    factor = jnp.linalg.cholesky(gram)
    coefficient = -jax.scipy.linalg.cho_solve((factor, True), projection)
    update = jnp.dot(
        coefficient, secant_w.reshape(columns, 3 * capacity), precision=lax.Precision.HIGHEST
    ).reshape(3, capacity)
    coupled = occupied[None, :] * (owned + update)
    return (field, coupled)


def solution(mesh):
    placed = (
        P("gx", "gy", None),
        P("gx", "gy", None),
        P("gx", "gy", None),
        P(None, ("gx", "gy")),
        P(None, ("gx", "gy")),
        P("gx", None),
        P(("gx", "gy")),
        P(None, ("gx", "gy")),
        P(None, None, ("gx", "gy")),
        P(None, None, ("gx", "gy")),
    )
    return jax.shard_map(
        shards,
        mesh=mesh,
        in_specs=placed,
        out_specs=(P("gx", "gy", None), P(None, ("gx", "gy"))),
        check_vma=False,
    )
```

profile of v0, /device:TPU:1, one launch (start us, length us, event | category | flops | bytes accessed | tf_op | source)
XLA Modules:
  0.0 306.0 jit_solution(7569810159518206231)
XLA Ops:
  0.6 0.0 copy-start
  0.6 0.9 fusion.35
  1.6 5.1 %collective-permute-start = (f32[1,16,512]{2,0,1:T(1,128)S(1)}, f32[1,16,512]{2,0,1:T(1,128)S(1)}, u32[]{:S(2)}, u32[]{:S(2)}) collective-permute-start(f32[1,16,512]{2,0,1:T(1,128)S(1)} %copy.23), channel_id=1, source_target_pairs={{32,0},{64,32},{96,64},{128,96},{160,128},{192,160},{224,192},{33,... | collective-permute-start | bytes 98312 | tf_op jit(solution)/shard_map/ppermute | solution.py:19
  6.7 1.9 collective-permute-start.1
  8.6 2.8 copy.24
  11.6 1.4 collective-permute-start.2
  13.0 4.0 %collective-permute-start.3 = (f32[66,1,512]{2,0,1:T(8,128)S(1)}, f32[66,1,512]{2,0,1:T(8,128)S(1)}, u32[]{:S(2)}, u32[]{:S(2)}) collective-permute-start(f32[66,1,512]{2,0,1:T(8,128)S(1)} %get-tuple-element.12), channel_id=1, source_target_pairs={{0,1},{1,2},{2,3},{3,4},{4,5},{5,6},{6,7},{7,8},{8,9},{9,10},{10,1... | collective-permute-start | bytes 405512 | tf_op jit(solution)/shard_map/ppermute | solution.py:17
  17.0 1.8 compare_select_fusion
  19.4 0.0 copy-start.2
  19.5 0.0 copy-start.4
  19.5 2.8 select_maximum_fusion.4
  22.4 0.0 copy-start.8
  22.4 6.9 %fusion.7 = f32[64,16,512]{2,0,1:T(8,128)S(1)} fusion(f32[66,18,514]{2,0,1:T(8,128)S(1)} %select_maximum_fusion.4, f32[66,1,512]{2,0,1:T(8,128)S(1)} %collective-permute-done.3, f32[1,16,512]{2,0,1:T(1,128)S(1)} %collective-permute-done, f32[64,16,512]{2,0,1:T(8,128)} %copy-done.1, f32[1,16,512]{2,0,1:T(1,128)S(1)} %collective-permute-done.1, ...), kind=kLoop, calls=%fused_computation.29 | loop fusion | flops 8388608 | bytes 12918784 | tf_op jit(solution)/shard_map/div | solution.py:36
  29.3 0.1 fusion.34
  29.3 3.4 %collective-permute-start.4 = (f32[1,16,512]{2,0,1:T(1,128)S(1)}, f32[1,16,512]{2,0,1:T(1,128)S(1)}, u32[]{:S(2)}, u32[]{:S(2)}) collective-permute-start(f32[1,16,512]{2,0,1:T(1,128)S(1)} %get-tuple-element.15), channel_id=1, source_target_pairs={{32,0},{64,32},{96,64},{128,96},{160,128},{192,160},{224,192},{33,... | collective-permute-start | bytes 98312 | tf_op jit(solution)/shard_map/ppermute | solution.py:19
  32.8 2.6 collective-permute-start.5
  35.4 1.7 copy.35
  37.1 1.4 collective-permute-start.6
  38.5 4.9 %collective-permute-start.7 = (f32[66,1,512]{2,0,1:T(8,128)S(1)}, f32[66,1,512]{2,0,1:T(8,128)S(1)}, u32[]{:S(2)}, u32[]{:S(2)}) collective-permute-start(f32[66,1,512]{2,0,1:T(8,128)S(1)} %get-tuple-element.10), channel_id=1, source_target_pairs={{0,1},{1,2},{2,3},{3,4},{4,5},{5,6},{6,7},{7,8},{8,9},{9,10},{10,1... | collective-permute-start | bytes 405512 | tf_op jit(solution)/shard_map/ppermute | solution.py:17
  43.5 1.1 convolution_bitcast_fusion
  44.5 0.0 copy-start.3
  44.6 1.1 collective-permute-done.6
  45.7 0.9 collective-permute-done.7
  46.6 2.8 select_maximum_fusion
  49.5 6.7 %fusion.2 = f32[64,16,512]{2,0,1:T(8,128)S(1)} fusion(f32[66,18,514]{2,0,1:T(8,128)S(1)} %select_maximum_fusion, f32[66,1,512]{2,0,1:T(8,128)S(1)} %collective-permute-done.7, f32[1,16,512]{2,0,1:T(1,128)S(1)} %collective-permute-done.4, f32[64,16,512]{2,0,1:T(8,128)S(1)} %fusion.7, f32[1,16,512]{2,0,1:T(1,128)S(1)} %collective-permute-done.5, ...), kind=kLoop, calls=%fused_computation.14 | loop fusion | flops 8388608 | bytes 12918784 | tf_op jit(solution)/shard_map/div | solution.py:36
  56.2 0.2 slice.128
  56.4 2.5 copy.37
  59.0 0.5 copy.31
  59.5 0.1 mul.33
  59.5 0.0 copy-done.10
  59.6 48.0 %all_gather.3 = f32[3,32768]{1,0:T(4,128)S(1)} all-gather(f32[3,1024]{1,0:T(4,128)S(1)} %multiply_add_fusion), channel_id=1, replica_groups=mesh['gx'=8,'gy'=32] {'gy'}, dimensions={1}, use_global_device_ids=true | all-gather | bytes 405504 | tf_op jit(solution)/shard_map/all_gather | solution.py:55
  107.6 8.5 %copy.32 = f32[32768,3]{1,0:T(8,128)} copy(f32[32768,3]{0,1:T(4,128)S(1)} %bitcast.77) | data formatting | bytes 786432 | tf_op jit(solution)/shard_map/all_gather | solution.py:55
  116.1 80.8 %scatter_custom_fusion = f32[3,3072]{0,1:T(8,128)S(1)} fusion(s32[32768]{0:T(1024)} %bitcast.78, f32[32768,3]{1,0:T(8,128)} %copy.32, f32[]{:T(128)} %constant.70.clone.1), kind=kCustom, calls=%fused_computation.58 | custom fusion | bytes 37376 | tf_op jit(solution)/shard_map/scatter | solution.py:57
  196.9 3.0 multiply_bitcast_fusion
  200.0 1.9 copy.40
  201.8 2.3 fusion.20
  204.1 86.8 %all-reduce.2 = (f32[32,32]{0,1:T(8,128)S(1)}, f32[32]{0:T(128)S(1)}) all-reduce(f32[32,32]{0,1:T(8,128)S(1)} %convolution_bitcast_fusion, f32[32]{0:T(128)S(1)} %fusion.20), channel_id=1, replica_groups=mesh['gx'=8,'gy'=32] {'gx','gy'}, use_global_device_ids=true, to_apply=%region_1.2 | all-reduce | flops 1056 | bytes 8448 | tf_op jit(solution)/shard_map/psum | solution.py:62
  291.0 0.1 copy.34
  291.1 2.9 cholesky.16
  294.0 0.6 compare_reduce_fusion
  294.7 0.7 fusion.28
  295.3 2.4 custom-call.10
  297.7 0.2 convolution_bitcast_fusion.2
  297.9 0.1 fusion.19
  298.1 0.7 fusion.12
  298.7 1.7 copy.42
  300.4 3.0 fusion.11
  303.5 2.5 copy.38
  (30 shorter events, 0.2 us)
Async XLA Ops:
  0.6 297.4 %copy-start = (f32[32,3,3072]{2,0,1:T(8,128)S(1)}, f32[32,3,3072]{2,0,1:T(8,128)}, u32[]{:S(2)}) copy-start(f32[32,3,3072]{2,0,1:T(8,128)} %param.19) | copy-start | bytes 3538948
  1.6 9.9 %collective-permute-start = (f32[1,16,512]{2,0,1:T(1,128)S(1)}, f32[1,16,512]{2,0,1:T(1,128)S(1)}, u32[]{:S(2)}, u32[]{:S(2)}) collective-permute-start(f32[1,16,512]{2,0,1:T(1,128)S(1)} %copy.23), channel_id=1, source_target_pairs={{32,0},{64,32},{96,64},{128,96},{160,128},{192,160},{224,192},{33,... | collective-permute-start | bytes 98312 | tf_op jit(solution)/shard_map/ppermute | solution.py:19
  6.7 4.8 %collective-permute-start.1 = (f32[1,16,512]{2,0,1:T(1,128)S(1)}, f32[1,16,512]{2,0,1:T(1,128)S(1)}, u32[]{:S(2)}, u32[]{:S(2)}) collective-permute-start(f32[1,16,512]{2,0,1:T(1,128)S(1)} %copy.25), channel_id=1, source_target_pairs={{0,32},{32,64},{64,96},{96,128},{128,160},{160,192},{192,224},{1,3... | collective-permute-start | bytes 98312 | tf_op jit(solution)/shard_map/ppermute | solution.py:17
  11.5 8.0 %copy-start.1 = (f32[64,16,512]{2,0,1:T(8,128)}, f32[64,16,512]{2,0,1:T(8,128)S(1)}, u32[]{:S(2)}) copy-start(f32[64,16,512]{2,0,1:T(8,128)S(1)} %copy.24) | copy-start | bytes 6291460
  11.5 5.5 %copy-start.7 = (s32[1,32768]{1,0:T(1,128)S(1)}, s32[1,32768]{1,0:T(1,128)}, u32[]{:S(2)}) copy-start(s32[1,32768]{1,0:T(1,128)} %param.15) | copy-start | bytes 393220
  11.6 7.9 %collective-permute-start.2 = (f32[66,1,512]{2,0,1:T(8,128)S(1)}, f32[66,1,512]{2,0,1:T(8,128)S(1)}, u32[]{:S(2)}, u32[]{:S(2)}) collective-permute-start(f32[66,1,512]{2,0,1:T(8,128)S(1)} %get-tuple-element.13), channel_id=1, source_target_pairs={{1,0},{2,1},{3,2},{4,3},{5,4},{6,5},{7,6},{8,7},{9,8},{10,9},{11,1... | collective-permute-start | bytes 405512 | tf_op jit(solution)/shard_map/ppermute | solution.py:19
  13.0 6.5 %collective-permute-start.3 = (f32[66,1,512]{2,0,1:T(8,128)S(1)}, f32[66,1,512]{2,0,1:T(8,128)S(1)}, u32[]{:S(2)}, u32[]{:S(2)}) collective-permute-start(f32[66,1,512]{2,0,1:T(8,128)S(1)} %get-tuple-element.12), channel_id=1, source_target_pairs={{0,1},{1,2},{2,3},{3,4},{4,5},{5,6},{6,7},{7,8},{8,9},{9,10},{10,1... | collective-permute-start | bytes 405512 | tf_op jit(solution)/shard_map/ppermute | solution.py:17
  19.4 2.9 copy-start.2
  19.5 2.9 copy-start.4
  22.4 13.0 %copy-start.8 = (f32[3,3072]{1,0:T(4,128)S(1)}, f32[3,3072]{1,0:T(4,128)}, u32[]{:S(2)}) copy-start(f32[3,3072]{1,0:T(4,128)} %param.17) | copy-start | bytes 110596
  29.3 7.7 %collective-permute-start.4 = (f32[1,16,512]{2,0,1:T(1,128)S(1)}, f32[1,16,512]{2,0,1:T(1,128)S(1)}, u32[]{:S(2)}, u32[]{:S(2)}) collective-permute-start(f32[1,16,512]{2,0,1:T(1,128)S(1)} %get-tuple-element.15), channel_id=1, source_target_pairs={{32,0},{64,32},{96,64},{128,96},{160,128},{192,160},{224,192},{33,... | collective-permute-start | bytes 98312 | tf_op jit(solution)/shard_map/ppermute | solution.py:19
  32.8 4.3 %collective-permute-start.5 = (f32[1,16,512]{2,0,1:T(1,128)S(1)}, f32[1,16,512]{2,0,1:T(1,128)S(1)}, u32[]{:S(2)}, u32[]{:S(2)}) collective-permute-start(f32[1,16,512]{2,0,1:T(1,128)S(1)} %get-tuple-element.14), channel_id=1, source_target_pairs={{0,32},{32,64},{64,96},{96,128},{128,160},{160,192},{192,224},{1,3... | collective-permute-start | bytes 98312 | tf_op jit(solution)/shard_map/ppermute | solution.py:17
  37.0 6.4 %copy-start.6 = (f32[32,3,3072]{2,0,1:T(8,128)S(1)}, f32[32,3,3072]{2,0,1:T(8,128)}, u32[]{:S(2)}) copy-start(f32[32,3,3072]{2,0,1:T(8,128)} %param.18) | copy-start | bytes 3538948
  37.1 8.6 %collective-permute-start.6 = (f32[66,1,512]{2,0,1:T(8,128)S(1)}, f32[66,1,512]{2,0,1:T(8,128)S(1)}, u32[]{:S(2)}, u32[]{:S(2)}) collective-permute-start(f32[66,1,512]{2,0,1:T(8,128)S(1)} %get-tuple-element.11), channel_id=1, source_target_pairs={{1,0},{2,1},{3,2},{4,3},{5,4},{6,5},{7,6},{8,7},{9,8},{10,9},{11,1... | collective-permute-start | bytes 405512 | tf_op jit(solution)/shard_map/ppermute | solution.py:19
  38.5 8.1 %collective-permute-start.7 = (f32[66,1,512]{2,0,1:T(8,128)S(1)}, f32[66,1,512]{2,0,1:T(8,128)S(1)}, u32[]{:S(2)}, u32[]{:S(2)}) collective-permute-start(f32[66,1,512]{2,0,1:T(8,128)S(1)} %get-tuple-element.10), channel_id=1, source_target_pairs={{0,1},{1,2},{2,3},{3,4},{4,5},{5,6},{6,7},{7,8},{8,9},{9,10},{10,1... | collective-permute-start | bytes 405512 | tf_op jit(solution)/shard_map/ppermute | solution.py:17
  44.5 4.9 %copy-start.3 = (f32[64,16,512]{2,1,0:T(8,128)S(1)}, f32[64,16,512]{2,1,0:T(8,128)}, u32[]{:S(2)}) copy-start(f32[64,16,512]{2,1,0:T(8,128)} %param.11) | copy-start | bytes 6291460
  44.6 4.9 %copy-start.5 = (f32[64,16,512]{2,1,0:T(8,128)S(1)}, f32[64,16,512]{2,1,0:T(8,128)}, u32[]{:S(2)}) copy-start(f32[64,16,512]{2,1,0:T(8,128)} %param.12) | copy-start | bytes 6291460
  56.4 3.1 %copy-start.9 = (f32[3,1024]{1,0:T(4,128)S(1)}, f32[3,1024]{1,0:T(4,128)}, u32[]{:S(2)}) copy-start(f32[3,1024]{1,0:T(4,128)} %param.14) | copy-start | bytes 36868
  56.4 3.1 %copy-start.10 = (f32[3,1024]{1,0:T(4,128)S(1)}, f32[3,1024]{1,0:T(4,128)}, u32[]{:S(2)}) copy-start(f32[3,1024]{1,0:T(4,128)} %param.13) | copy-start | bytes 36868
where the time goes:
time: 307 us; the launch traced here: 306 us
  blocking collectives  135 us (44%)
  local copies, waits for them, and re-layouts  104 us (34%)
  other arithmetic  33.9 us (11%)
  starting transfers between devices  24.8 us (8%)
  matrix products  4.35 us (1%)
    psum x1, blocking collectives, shards(): gram, projection = lax.psum((gram_local, projection_local), ('gx', 'gy'))  86.8 us
    scatter x1, local copies, waits for them, and re-layouts, shards(): jnp.zeros((3, capacity), jnp.float32).at[:, placed]  80.8 us
    all_gather x1, blocking collectives, shards(): gathered = lax.all_gather(forces, 'gy', axis=1, tiled=True)  48 us
    div x2, other arithmetic, sweep_once(): return (divergence + stencil_sum(padded)) / (6.0 + diagonal)  13.6 us
    ppermute x4, starting transfers between devices, extended(): lax.ppermute(tail, axis, [(i, (i + 1) % count) for i in range(ends)])  13.4 us
    ppermute x4, starting transfers between devices, extended(): lax.ppermute(head, axis, [((i + 1) % count, i) for i in range(ends)])  11.4 us
    unnamed x26, local copies, waits for them, and re-layouts  9.59 us
    all_gather x1, local copies, waits for them, and re-layouts, shards(): gathered = lax.all_gather(forces, 'gy', axis=1, tiled=True)  8.53 us
  transfers between devices with their start and end apart: 8, of which 2 were waited for; matrix products, arithmetic and copies ran while one was open for 2% of the time, Pallas kernels for 0%

commit v1 on v0

--- a/solution.py
+++ b/solution.py
@@ -52,7 +52,20 @@
     forces = normals * surface[None, :] + traction
     own_index = lax.axis_index("gy")
     all_slots = slot_of[0]
-    gathered = lax.all_gather(forces, "gy", axis=1, tiled=True)
+    long_array = lax.axis_index("gy")
+    field_out = lax.axis_size("gy")
+    w2, found_now, piece_now = (field_out, long_array, forces.shape[1])
+    local_part, a_now = (forces, 1)
+    while a_now < w2:
+        buffer = []
+        num = 0
+        while num < w2:
+            buffer.append((num, (num - a_now) % w2))
+            num += 1
+        y1 = lax.ppermute(local_part, axis_name="gy", perm=buffer)
+        local_part = jnp.concatenate([local_part, y1], axis=1)
+        a_now = 2 * a_now
+    gathered = jnp.roll(local_part, found_now * piece_now, 1)
     placed = jnp.where(all_slots // capacity == own_index, all_slots % capacity, capacity)
     owned = jnp.zeros((3, capacity), jnp.float32).at[:, placed].set(gathered, mode="drop")
     residual = occupied[None, :] * (owned - previous)

time: 307 us -> 300 us (0.977)
  blocking collectives: 135 us -> 88 us
  starting transfers between devices: 24.8 us -> 49.3 us
  waiting for transfers between devices: 2.07 us -> 8.8 us
  local copies, waits for them, and re-layouts: 104 us -> 110 us
    all_gather x1 -> x0, blocking collectives: 48 us -> none  [shards(): gathered = lax.all_gather(forces, 'gy', axis=1, tiled=True)]
    ppermute x0 -> x5, starting transfers between devices: none -> 24.4 us  [shards(): y1 = lax.ppermute(local_part, axis_name='gy', perm=buffer)]
    dynamic_slice x0 -> x2, local copies, waits for them, and re-layouts: none -> 8.59 us  [shards(): gathered = jnp.roll(local_part, found_now * piece_now, 1)]
    all_gather x1 -> x0, local copies, waits for them, and re-layouts: 8.53 us -> none  [shards(): gathered = lax.all_gather(forces, 'gy', axis=1, tiled=True)]
    unnamed x26 -> x56, local copies, waits for them, and re-layouts: 9.59 us -> 14.4 us
    ppermute x0 -> x5, waiting for transfers between devices: none -> 4.58 us  [shards(): y1 = lax.ppermute(local_part, axis_name='gy', perm=buffer)]
  transfers between devices with their start and end apart: 8 -> 13, of which waited for: 2 -> 8; matrix products, arithmetic and copies ran while one was open for 2% -> 5% of each run, Pallas kernels for 0% -> 0%
where the time goes in v1:
time: 300 us
  local copies, waits for them, and re-layouts  110 us (37%)
  blocking collectives  88 us (29%)
  starting transfers between devices  49.3 us (16%)
  other arithmetic  35.1 us (12%)
  waiting for transfers between devices  8.8 us (3%)
  matrix products  6.78 us (2%)
    psum x1, blocking collectives, shards(): gram, projection = lax.psum((gram_local, projection_local), ('gx', 'gy'))  88 us
    scatter x1, local copies, waits for them, and re-layouts, shards(): jnp.zeros((3, capacity), jnp.float32).at[:, placed]  80.8 us
    ppermute x5, starting transfers between devices, shards(): y1 = lax.ppermute(local_part, axis_name='gy', perm=buffer)  24.4 us
    unnamed x56, local copies, waits for them, and re-layouts  14.4 us
    ppermute x4, starting transfers between devices, extended(): lax.ppermute(tail, axis, [(i, (i + 1) % count) for i in range(ends)])  13.7 us
    div x2, other arithmetic, sweep_once(): return (divergence + stencil_sum(padded)) / (6.0 + diagonal)  13.5 us
    ppermute x4, starting transfers between devices, extended(): lax.ppermute(head, axis, [((i + 1) % count, i) for i in range(ends)])  11.2 us
    dynamic_slice x2, local copies, waits for them, and re-layouts, shards(): gathered = jnp.roll(local_part, found_now * piece_now, 1)  8.59 us
  transfers between devices with their start and end apart: 13, of which 8 were waited for; matrix products, arithmetic and copies ran while one was open for 5% of the time, Pallas kernels for 0%

profile of v1, /device:TPU:1, one launch (start us, length us, event | category | flops | bytes accessed | tf_op | source)
XLA Modules:
  0.0 299.8 jit_solution(8713053610088804036)
XLA Ops:
  0.6 0.9 fusion.35
  1.6 5.1 %collective-permute-start = (f32[1,16,512]{2,0,1:T(1,128)S(1)}, f32[1,16,512]{2,0,1:T(1,128)S(1)}, u32[]{:S(2)}, u32[]{:S(2)}) collective-permute-start(f32[1,16,512]{2,0,1:T(1,128)S(1)} %copy.23), channel_id=1, source_target_pairs={{32,0},{64,32},{96,64},{128,96},{160,128},{192,160},{224,192},{33,... | collective-permute-start | bytes 98312 | tf_op jit(solution)/shard_map/ppermute | solution.py:19
  6.7 1.9 collective-permute-start.1
  8.6 2.8 copy.24
  11.5 1.3 collective-permute-start.2
  12.8 4.3 %collective-permute-start.3 = (f32[66,1,512]{2,0,1:T(8,128)S(1)}, f32[66,1,512]{2,0,1:T(8,128)S(1)}, u32[]{:S(2)}, u32[]{:S(2)}) collective-permute-start(f32[66,1,512]{2,0,1:T(8,128)S(1)} %get-tuple-element.14), channel_id=1, source_target_pairs={{0,1},{1,2},{2,3},{3,4},{4,5},{5,6},{6,7},{7,8},{8,9},{9,10},{10,1... | collective-permute-start | bytes 405512 | tf_op jit(solution)/shard_map/ppermute | solution.py:17
  17.1 1.2 collective-permute-done.2
  18.3 1.2 collective-permute-done.3
  19.5 2.8 select_maximum_fusion.4
  22.4 6.8 %fusion.7 = f32[64,16,512]{2,0,1:T(8,128)S(1)} fusion(f32[66,18,514]{2,0,1:T(8,128)S(1)} %select_maximum_fusion.4, f32[66,1,512]{2,0,1:T(8,128)S(1)} %collective-permute-done.3, f32[1,16,512]{2,0,1:T(1,128)S(1)} %collective-permute-done, f32[64,16,512]{2,0,1:T(8,128)S(1)} %copy.24, f32[1,16,512]{2,0,1:T(1,128)S(1)} %collective-permute-done.1, ...), kind=kLoop, calls=%fused_computation.29 | loop fusion | flops 8388608 | bytes 12918784 | tf_op jit(solution)/shard_map/div | solution.py:36
  29.3 3.5 %collective-permute-start.4 = (f32[1,16,512]{2,0,1:T(1,128)S(1)}, f32[1,16,512]{2,0,1:T(1,128)S(1)}, u32[]{:S(2)}, u32[]{:S(2)}) collective-permute-start(f32[1,16,512]{2,0,1:T(1,128)S(1)} %get-tuple-element.17), channel_id=1, source_target_pairs={{32,0},{64,32},{96,64},{128,96},{160,128},{192,160},{224,192},{33,... | collective-permute-start | bytes 98312 | tf_op jit(solution)/shard_map/ppermute | solution.py:19
  32.8 2.6 collective-permute-start.5
  35.4 1.0 collective-permute-done.5
  36.4 1.3 collective-permute-start.6
  37.7 4.9 %collective-permute-start.7 = (f32[66,1,512]{2,0,1:T(8,128)S(1)}, f32[66,1,512]{2,0,1:T(8,128)S(1)}, u32[]{:S(2)}, u32[]{:S(2)}) collective-permute-start(f32[66,1,512]{2,0,1:T(8,128)S(1)} %get-tuple-element.12), channel_id=1, source_target_pairs={{0,1},{1,2},{2,3},{3,4},{4,5},{5,6},{6,7},{7,8},{8,9},{9,10},{10,1... | collective-permute-start | bytes 405512 | tf_op jit(solution)/shard_map/ppermute | solution.py:17
  42.7 1.8 compare_select_fusion
  45.2 0.8 collective-permute-done.7
  46.0 2.8 select_maximum_fusion
  48.9 6.7 %fusion.2 = f32[64,16,512]{2,0,1:T(8,128)S(1)} fusion(f32[66,18,514]{2,0,1:T(8,128)S(1)} %select_maximum_fusion, f32[66,1,512]{2,0,1:T(8,128)S(1)} %collective-permute-done.7, f32[1,16,512]{2,0,1:T(1,128)S(1)} %collective-permute-done.4, f32[64,16,512]{2,0,1:T(8,128)S(1)} %fusion.7, f32[1,16,512]{2,0,1:T(1,128)S(1)} %collective-permute-done.5, ...), kind=kLoop, calls=%fused_computation.14 | loop fusion | flops 8388608 | bytes 12918784 | tf_op jit(solution)/shard_map/div | solution.py:36
  55.6 1.3 copy-done.1
  58.3 9.1 %collective-permute-start.8 = (f32[3,1024]{1,0:T(4,128)S(1)}, f32[3,1024]{1,0:T(4,128)S(1)}, u32[]{:S(2)}, u32[]{:S(2)}) collective-permute-start(f32[3,1024]{1,0:T(4,128)S(1)} %get-tuple-element.11), channel_id=1, source_target_pairs={{0,31},{1,0},{2,1},{3,2},{4,3},{5,4},{6,5},{7,6},{8,7},{9,8},{10,9... | collective-permute-start | bytes 36872 | tf_op jit(solution)/shard_map/ppermute | solution.py:65
  68.3 5.1 %collective-permute-start.9 = (f32[3,2048]{1,0:T(4,128)S(1)}, f32[3,2048]{1,0:T(4,128)S(1)}, u32[]{:S(2)}, u32[]{:S(2)}) collective-permute-start(f32[3,2048]{1,0:T(4,128)S(1)} %pad_maximum_fusion.24), channel_id=1, source_target_pairs={{0,30},{1,31},{2,0},{3,1},{4,2},{5,3},{6,4},{7,5},{8,6},{9,7},{10,... | collective-permute-start | bytes 73736 | tf_op jit(solution)/shard_map/ppermute | solution.py:65
  73.4 0.6 constant_dynamic-update-slice_fusion.3
  74.4 3.8 %collective-permute-start.10 = (f32[3,4096]{1,0:T(4,128)S(1)}, f32[3,4096]{1,0:T(4,128)S(1)}, u32[]{:S(2)}, u32[]{:S(2)}) collective-permute-start(f32[3,4096]{1,0:T(4,128)S(1)} %pad_maximum_fusion.23), channel_id=1, source_target_pairs={{0,28},{1,29},{2,30},{3,31},{4,0},{5,1},{6,2},{7,3},{8,4},{9,5},{1... | collective-permute-start | bytes 147464 | tf_op jit(solution)/shard_map/ppermute | solution.py:65
  78.3 0.6 constant_dynamic-update-slice_fusion.2
  78.9 0.7 collective-permute-done.10
  79.6 2.3 collective-permute-start.11
  82.0 0.7 constant_dynamic-update-slice_fusion.1
  82.6 3.2 %collective-permute-done.11 = f32[3,8192]{1,0:T(4,128)S(1)} collective-permute-done((f32[3,8192]{1,0:T(4,128)S(1)}, f32[3,8192]{1,0:T(4,128)S(1)}, u32[]{:S(2)}, u32[]{:S(2)}) %collective-permute-start.11) | collective-permute-done | bytes 98336 | tf_op jit(solution)/shard_map/ppermute | solution.py:65
  85.8 0.7 constant_dynamic-update-slice_fusion
  86.6 4.1 %collective-permute-start.12 = (f32[3,16384]{1,0:T(4,128)}, f32[3,16384]{1,0:T(4,128)S(1)}, u32[]{:S(2)}, u32[]{:S(2)}) collective-permute-start(f32[3,16384]{1,0:T(4,128)} %get-tuple-element.20), channel_id=1, source_target_pairs={{0,16},{1,17},{2,18},{3,19},{4,20},{5,21},{6,22},{7,23},{8,24},{9,... | collective-permute-start | bytes 589832 | tf_op jit(solution)/shard_map/ppermute | solution.py:65
  91.2 2.5 copy.35
  93.7 3.5 %convolution_bitcast_fusion = f32[32,32]{0,1:T(8,128)} fusion(f32[32,3,3072]{2,0,1:T(8,128)} %param.18, f32[3072]{0:T(1024)} %fusion.32), kind=kOutput, calls=%fused_computation.49 | convolution fusion | flops 113541120 | bytes 1196032 | tf_op jit(solution)/shard_map/dot_general | solution.py:47
  97.3 2.5 copy.37
  100.2 8.5 %copy.32 = f32[32768,3]{1,0:T(8,128)} copy(f32[32768,3]{0,1:T(4,128)S(1)} %dynamic-slice_bitcast_fusion) | data formatting | bytes 786432 | tf_op jit(solution)/shard_map/jit(_roll_dynamic)/dynamic_slice | solution.py:68
  108.7 80.8 %scatter_custom_fusion = f32[3,3072]{0,1:T(8,128)S(1)} fusion(s32[32768]{0:T(1024)} %bitcast.78, f32[32768,3]{1,0:T(8,128)} %copy.32, f32[]{:T(128)} %constant.89.clone.1), kind=kCustom, calls=%fused_computation.58 | custom fusion | bytes 37376 | tf_op jit(solution)/shard_map/scatter | solution.py:70
  189.5 3.1 %multiply_bitcast_fusion = f32[3,3072,1]{0,1,2:T(8,128)} fusion(f32[3,3072]{0,1:T(8,128)S(1)} %scatter_custom_fusion, f32[3,3072]{0,1:T(8,128)} %copy.35, f32[3072]{0:T(1024)S(1)} %copy-done.15), kind=kLoop, calls=%fused_computation.45 | loop fusion | flops 18432 | bytes 122880 | tf_op jit(solution)/shard_map/mul | solution.py:71
  192.6 1.9 copy.40
  194.5 2.3 fusion.20
  196.8 88.0 %all-reduce.2 = (f32[32,32]{0,1:T(8,128)S(1)}, f32[32]{0:T(128)S(1)}) all-reduce(f32[32,32]{0,1:T(8,128)S(1)} %copy-done.18, f32[32]{0:T(128)S(1)} %fusion.20), channel_id=1, replica_groups=mesh['gx'=8,'gy'=32] {'gx','gy'}, use_global_device_ids=true, to_apply=%region_1.2 | all-reduce | flops 1056 | bytes 8448 | tf_op jit(solution)/shard_map/psum | solution.py:75
  284.8 2.9 cholesky.16
  287.8 0.6 compare_reduce_fusion
  288.4 0.7 fusion.28
  289.1 2.4 custom-call.10
  291.8 0.7 fusion.12
  292.5 1.7 copy.42
  294.2 3.1 %fusion.11 = f32[3,3072]{0,1:T(8,128)} fusion(f32[3,3072]{0,1:T(8,128)S(1)} %scatter_custom_fusion, f32[1,3,3072]{1,2,0:T(8,128)} %copy.42, f32[3072]{0:T(1024)S(1)} %copy-done.15), kind=kLoop, calls=%fused_computation.44 | loop fusion | flops 18432 | bytes 122880 | tf_op jit(solution)/shard_map/mul | solution.py:81
  297.3 2.5 copy.38
  (75 shorter events, 4.3 us)
Async XLA Ops:
  0.6 291.2 %copy-start = (f32[32,3,3072]{2,0,1:T(8,128)S(1)}, f32[32,3,3072]{2,0,1:T(8,128)}, u32[]{:S(2)}) copy-start(f32[32,3,3072]{2,0,1:T(8,128)} %param.19) | copy-start | bytes 3538948
  1.6 9.9 %collective-permute-start = (f32[1,16,512]{2,0,1:T(1,128)S(1)}, f32[1,16,512]{2,0,1:T(1,128)S(1)}, u32[]{:S(2)}, u32[]{:S(2)}) collective-permute-start(f32[1,16,512]{2,0,1:T(1,128)S(1)} %copy.23), channel_id=1, source_target_pairs={{32,0},{64,32},{96,64},{128,96},{160,128},{192,160},{224,192},{33,... | collective-permute-start | bytes 98312 | tf_op jit(solution)/shard_map/ppermute | solution.py:19
  6.7 4.8 %collective-permute-start.1 = (f32[1,16,512]{2,0,1:T(1,128)S(1)}, f32[1,16,512]{2,0,1:T(1,128)S(1)}, u32[]{:S(2)}, u32[]{:S(2)}) collective-permute-start(f32[1,16,512]{2,0,1:T(1,128)S(1)} %copy.25), channel_id=1, source_target_pairs={{0,32},{32,64},{64,96},{96,128},{128,160},{160,192},{192,224},{1,3... | collective-permute-start | bytes 98312 | tf_op jit(solution)/shard_map/ppermute | solution.py:17
  11.5 6.8 %collective-permute-start.2 = (f32[66,1,512]{2,0,1:T(8,128)S(1)}, f32[66,1,512]{2,0,1:T(8,128)S(1)}, u32[]{:S(2)}, u32[]{:S(2)}) collective-permute-start(f32[66,1,512]{2,0,1:T(8,128)S(1)} %get-tuple-element.15), channel_id=1, source_target_pairs={{1,0},{2,1},{3,2},{4,3},{5,4},{6,5},{7,6},{8,7},{9,8},{10,9},{11,1... | collective-permute-start | bytes 405512 | tf_op jit(solution)/shard_map/ppermute | solution.py:19
  12.8 9.5 %copy-start.3 = (f32[64,16,512]{2,1,0:T(8,128)S(1)}, f32[64,16,512]{2,1,0:T(8,128)}, u32[]{:S(2)}) copy-start(f32[64,16,512]{2,1,0:T(8,128)} %param.11) | copy-start | bytes 6291460
  12.8 9.5 %copy-start.5 = (f32[64,16,512]{2,1,0:T(8,128)S(1)}, f32[64,16,512]{2,1,0:T(8,128)}, u32[]{:S(2)}) copy-start(f32[64,16,512]{2,1,0:T(8,128)} %param.12) | copy-start | bytes 6291460
  12.8 6.7 %collective-permute-start.3 = (f32[66,1,512]{2,0,1:T(8,128)S(1)}, f32[66,1,512]{2,0,1:T(8,128)S(1)}, u32[]{:S(2)}, u32[]{:S(2)}) collective-permute-start(f32[66,1,512]{2,0,1:T(8,128)S(1)} %get-tuple-element.14), channel_id=1, source_target_pairs={{0,1},{1,2},{2,3},{3,4},{4,5},{5,6},{6,7},{7,8},{8,9},{9,10},{10,1... | collective-permute-start | bytes 405512 | tf_op jit(solution)/shard_map/ppermute | solution.py:17
  29.2 13.5 %copy-start.17 = (s32[1,32768]{1,0:T(1,128)S(1)}, s32[1,32768]{1,0:T(1,128)}, u32[]{:S(2)}) copy-start(s32[1,32768]{1,0:T(1,128)} %param.15) | copy-start | bytes 393220
  29.3 6.1 %collective-permute-start.4 = (f32[1,16,512]{2,0,1:T(1,128)S(1)}, f32[1,16,512]{2,0,1:T(1,128)S(1)}, u32[]{:S(2)}, u32[]{:S(2)}) collective-permute-start(f32[1,16,512]{2,0,1:T(1,128)S(1)} %get-tuple-element.17), channel_id=1, source_target_pairs={{32,0},{64,32},{96,64},{128,96},{160,128},{192,160},{224,192},{33,... | collective-permute-start | bytes 98312 | tf_op jit(solution)/shard_map/ppermute | solution.py:19
  32.8 3.6 %collective-permute-start.5 = (f32[1,16,512]{2,0,1:T(1,128)S(1)}, f32[1,16,512]{2,0,1:T(1,128)S(1)}, u32[]{:S(2)}, u32[]{:S(2)}) collective-permute-start(f32[1,16,512]{2,0,1:T(1,128)S(1)} %get-tuple-element.16), channel_id=1, source_target_pairs={{0,32},{32,64},{64,96},{96,128},{128,160},{160,192},{192,224},{1,3... | collective-permute-start | bytes 98312 | tf_op jit(solution)/shard_map/ppermute | solution.py:17
  36.4 8.7 %collective-permute-start.6 = (f32[66,1,512]{2,0,1:T(8,128)S(1)}, f32[66,1,512]{2,0,1:T(8,128)S(1)}, u32[]{:S(2)}, u32[]{:S(2)}) collective-permute-start(f32[66,1,512]{2,0,1:T(8,128)S(1)} %get-tuple-element.13), channel_id=1, source_target_pairs={{1,0},{2,1},{3,2},{4,3},{5,4},{6,5},{7,6},{8,7},{9,8},{10,9},{11,1... | collective-permute-start | bytes 405512 | tf_op jit(solution)/shard_map/ppermute | solution.py:19
  37.7 8.2 %collective-permute-start.7 = (f32[66,1,512]{2,0,1:T(8,128)S(1)}, f32[66,1,512]{2,0,1:T(8,128)S(1)}, u32[]{:S(2)}, u32[]{:S(2)}) collective-permute-start(f32[66,1,512]{2,0,1:T(8,128)S(1)} %get-tuple-element.12), channel_id=1, source_target_pairs={{0,1},{1,2},{2,3},{3,4},{4,5},{5,6},{6,7},{7,8},{8,9},{9,10},{10,1... | collective-permute-start | bytes 405512 | tf_op jit(solution)/shard_map/ppermute | solution.py:17
  45.1 3.7 %copy-start.4 = (f32[64,16,512]{2,1,0:T(8,128)S(1)}, f32[64,16,512]{2,1,0:T(8,128)}, u32[]{:S(2)}) copy-start(f32[64,16,512]{2,1,0:T(8,128)} %param.11) | copy-start | bytes 6291460
  45.1 3.7 %copy-start.6 = (f32[64,16,512]{2,1,0:T(8,128)S(1)}, f32[64,16,512]{2,1,0:T(8,128)}, u32[]{:S(2)}) copy-start(f32[64,16,512]{2,1,0:T(8,128)} %param.12) | copy-start | bytes 6291460
  48.8 8.8 %copy-start.19 = (f32[3,1024]{1,0:T(4,128)S(1)}, f32[3,1024]{1,0:T(4,128)}, u32[]{:S(2)}) copy-start(f32[3,1024]{1,0:T(4,128)} %param.14) | copy-start | bytes 36868
  48.8 8.8 %copy-start.20 = (f32[3,1024]{1,0:T(4,128)S(1)}, f32[3,1024]{1,0:T(4,128)}, u32[]{:S(2)}) copy-start(f32[3,1024]{1,0:T(4,128)} %param.13) | copy-start | bytes 36868
  55.6 1.3 copy-start.1
  57.7 39.5 %copy-start.2 = (f32[64,16,512]{2,0,1:T(8,128)S(1)}, f32[64,16,512]{2,0,1:T(8,128)}, u32[]{:S(2)}) copy-start(f32[64,16,512]{2,0,1:T(8,128)} %copy-done.1) | copy-start | bytes 6291460
  58.3 10.0 %collective-permute-start.8 = (f32[3,1024]{1,0:T(4,128)S(1)}, f32[3,1024]{1,0:T(4,128)S(1)}, u32[]{:S(2)}, u32[]{:S(2)}) collective-permute-start(f32[3,1024]{1,0:T(4,128)S(1)} %get-tuple-element.11), channel_id=1, source_target_pairs={{0,31},{1,0},{2,1},{3,2},{4,3},{5,4},{6,5},{7,6},{8,7},{9,8},{10,9... | collective-permute-start | bytes 36872 | tf_op jit(solution)/shard_map/ppermute | solution.py:65
  68.3 11.3 %copy-start.13 = (f32[3,1024]{1,0:T(4,128)}, f32[3,1024]{1,0:T(4,128)S(1)}, u32[]{:S(2)}) copy-start(f32[3,1024]{1,0:T(4,128)S(1)} %collective-permute-done.8) | copy-start | bytes 36868
  68.3 6.1 %collective-permute-start.9 = (f32[3,2048]{1,0:T(4,128)S(1)}, f32[3,2048]{1,0:T(4,128)S(1)}, u32[]{:S(2)}, u32[]{:S(2)}) collective-permute-start(f32[3,2048]{1,0:T(4,128)S(1)} %pad_maximum_fusion.24), channel_id=1, source_target_pairs={{0,30},{1,31},{2,0},{3,1},{4,2},{5,3},{6,4},{7,5},{8,6},{9,7},{10,... | collective-permute-start | bytes 73736 | tf_op jit(solution)/shard_map/ppermute | solution.py:65
  74.4 5.2 %copy-start.11 = (f32[3,2048]{1,0:T(4,128)}, f32[3,2048]{1,0:T(4,128)S(1)}, u32[]{:S(2)}) copy-start(f32[3,2048]{1,0:T(4,128)S(1)} %collective-permute-done.9) | copy-start | bytes 73732
  74.4 5.2 %collective-permute-start.10 = (f32[3,4096]{1,0:T(4,128)S(1)}, f32[3,4096]{1,0:T(4,128)S(1)}, u32[]{:S(2)}, u32[]{:S(2)}) collective-permute-start(f32[3,4096]{1,0:T(4,128)S(1)} %pad_maximum_fusion.23), channel_id=1, source_target_pairs={{0,28},{1,29},{2,30},{3,31},{4,0},{5,1},{6,2},{7,3},{8,4},{9,5},{1... | collective-permute-start | bytes 147464 | tf_op jit(solution)/shard_map/ppermute | solution.py:65
  79.6 6.9 %copy-start.7 = (f32[3,4096]{1,0:T(4,128)}, f32[3,4096]{1,0:T(4,128)S(1)}, u32[]{:S(2)}) copy-start(f32[3,4096]{1,0:T(4,128)S(1)} %collective-permute-done.10) | copy-start | bytes 147460
  79.6 6.2 %collective-permute-start.11 = (f32[3,8192]{1,0:T(4,128)S(1)}, f32[3,8192]{1,0:T(4,128)S(1)}, u32[]{:S(2)}, u32[]{:S(2)}) collective-permute-start(f32[3,8192]{1,0:T(4,128)S(1)} %pad_maximum_fusion.22), channel_id=1, source_target_pairs={{0,24},{1,25},{2,26},{3,27},{4,28},{5,29},{6,30},{7,31},{8,0},{9,1... | collective-permute-start | bytes 294920 | tf_op jit(solution)/shard_map/ppermute | solution.py:65
  85.8 0.7 copy-start.9
  86.6 13.2 %collective-permute-start.12 = (f32[3,16384]{1,0:T(4,128)}, f32[3,16384]{1,0:T(4,128)S(1)}, u32[]{:S(2)}, u32[]{:S(2)}) collective-permute-start(f32[3,16384]{1,0:T(4,128)} %get-tuple-element.20), channel_id=1, source_target_pairs={{0,16},{1,17},{2,18},{3,19},{4,20},{5,21},{6,22},{7,23},{8,24},{9,... | collective-permute-start | bytes 589832 | tf_op jit(solution)/shard_map/ppermute | solution.py:65
  97.2 2.6 copy-start.16
  97.2 2.7 copy-start.14
  97.2 2.7 copy-start.12
  97.2 2.7 copy-start.8
  97.3 2.7 copy-start.10
  100.2 89.3 %copy-start.15 = (f32[3072]{0:T(1024)S(1)}, f32[3072]{0:T(1024)}, u32[]{:S(2)}) copy-start(f32[3072]{0:T(1024)} %fusion.32) | copy-start | bytes 36868
  192.6 4.2 %copy-start.18 = (f32[32,32]{0,1:T(8,128)S(1)}, f32[32,32]{0,1:T(8,128)}, u32[]{:S(2)}) copy-start(f32[32,32]{0,1:T(8,128)} %convolution_bitcast_fusion) | copy-start | bytes 12292
